TPU v7x, 32 devices: a whole 2x2x4 slice. The times are simulated.
32 devices in a mesh: dp: 8 (over y, x, core), mp: 4 (over z).
Axes of the slice: x: 2, y: 2, z: 4, core: 2. Of those that a mesh axis runs over, the one named last changes fastest.
Arguments:
- query_new: bfloat16 [32, 4096], P(('dp', 'mp')), parts along dimension 0, may hold values from -140 to 140
- key_new: bfloat16 [32, 1024], P(('dp', 'mp')), parts along dimension 0, may hold values from -5 to 5
- value_new: bfloat16 [32, 1024], P(('dp', 'mp')), parts along dimension 0, may hold values from -5 to 5
- prefix_keys: bfloat16 [4096, 1024], P(('dp', 'mp')), parts along dimension 0, may hold values from -5 to 5
- prefix_values: bfloat16 [4096, 1024], P(('dp', 'mp')), parts along dimension 0, may hold values from -5 to 5
- sample_suffix_keys: bfloat16 [32, 64, 1024], P(('dp', 'mp')), parts along dimension 0, may hold values from -5 to 5
- sample_suffix_values: bfloat16 [32, 64, 1024], P(('dp', 'mp')), parts along dimension 0, may hold values from -5 to 5
- prefix_len: int32 [8], P('dp'), parts along dimension 0, may hold values from 128 to 512
- suffix_len: int32 [32], P(('dp', 'mp')), parts along dimension 0, may hold values from 1 to 64, as said below
- residual: bfloat16 [32, 8192], P(('dp', 'mp')), parts along dimension 0, may hold values from -3 to 3
- out_weight: bfloat16 [4096, 8192], P('mp'), may hold values from -0.1875 to 0.1875
- norm_gain: bfloat16 [8192], replicated, may hold values from 0.5 to 1.5
Outputs:
- hidden: bfloat16 [32, 8192], P(('dp', 'mp')), parts along dimension 0
- normed: bfloat16 [32, 8192], P(('dp', 'mp')), parts along dimension 0
There are 8 independent parts, one for each index of `dp`. A program takes and returns all parts, laid end to end along the dimension named above; an argument that names none is the same for every part. Nothing has to cross between parts.
Inputs may be any that keep to these rules, and one draw needn't show every extreme that they name: `suffix_len`: some sample has exactly 64 cached generated tokens.
All inputs are finite; a program needn't handle non-finite values.
Results may differ from a plain program's by a relative error of at most 0.0085.
Values may be sent and summed in bfloat16 or wider, within the bound.
A program may use at most 64 MiB of HBM per device.

v0:
```python
import jax
import jax.numpy as jnp
from jax import lax
from jax.sharding import PartitionSpec as P

HEAD_SIZE = 128
KEY_VALUE_HEADS = 8
HQ = 32


def local(
    query_new,
    key_new,
    value_new,
    prefix_keys,
    prefix_values,
    sample_suffix_keys,
    sample_suffix_values,
    prefix_len,
    suffix_len,
    residual,
    out_weight,
    norm_gain,
):
    count_mp = lax.axis_size("mp")
    place = lax.axis_index("mp")
    samples_per_part = query_new.shape[0]
    batch = samples_per_part * count_mp
    heads_dev = out_weight.shape[0] // HEAD_SIZE
    group = HQ // KEY_VALUE_HEADS
    pre_dev = prefix_keys.shape[0]
    suffix_result = sample_suffix_keys.shape[1]
    score_scale = HEAD_SIZE ** (-0.5)
    first_row = place * samples_per_part
    queries = lax.all_gather(query_new, "mp", axis=0, tiled=True)
    query_all = queries.reshape(batch, KEY_VALUE_HEADS, group, HEAD_SIZE)
    pkeys = prefix_keys.reshape(pre_dev, KEY_VALUE_HEADS, HEAD_SIZE)
    prefix_value_rows = prefix_values.reshape(pre_dev, KEY_VALUE_HEADS, HEAD_SIZE)
    s_pre = (
        jnp.einsum("bkgd,pkd->bkgp", query_all, pkeys, preferred_element_type=jnp.float32)
        * score_scale
    )
    positions = place * pre_dev + lax.iota(jnp.int32, pre_dev)
    pvalid = (positions < prefix_len[0])[None, None, None, :]
    s_pre = jnp.where(pvalid, s_pre, -jnp.inf)
    query_sample_rows = query_new.reshape(samples_per_part, KEY_VALUE_HEADS, group, HEAD_SIZE)
    suffix_key_rows = sample_suffix_keys.reshape(
        samples_per_part, suffix_result, KEY_VALUE_HEADS, HEAD_SIZE
    )
    suffix_value_rows = sample_suffix_values.reshape(
        samples_per_part, suffix_result, KEY_VALUE_HEADS, HEAD_SIZE
    )
    nvals = value_new.reshape(samples_per_part, KEY_VALUE_HEADS, HEAD_SIZE)
    suffix_score_rows = (
        jnp.einsum(
            "cqxt,caqt->cqxa",
            query_sample_rows,
            suffix_key_rows,
            preferred_element_type=jnp.float32,
        )
        * score_scale
    )
    svalid = (lax.iota(jnp.int32, suffix_result)[None, :] < suffix_len[:, None])[:, None, None, :]
    suffix_score_rows = jnp.where(svalid, suffix_score_rows, -jnp.inf)
    fresh_score_rows = (
        jnp.einsum(
            "exio,exo->exi",
            query_sample_rows,
            key_new.reshape(samples_per_part, KEY_VALUE_HEADS, HEAD_SIZE),
            preferred_element_type=jnp.float32,
        )
        * score_scale
    )
    top_pre = jnp.maximum(jnp.max(s_pre, -1), -1e30)
    own_top = lax.dynamic_slice_in_dim(top_pre, first_row, samples_per_part, 0)
    own_top = jnp.maximum(jnp.maximum(own_top, jnp.max(suffix_score_rows, -1)), fresh_score_rows)
    local_top = lax.dynamic_update_slice_in_dim(top_pre, own_top, first_row, 0)
    top_own = lax.dynamic_slice_in_dim(local_top, first_row, samples_per_part, 0)
    w_pre = jnp.where(pvalid, jnp.exp(s_pre - local_top[..., None]), 0.0)
    total = jnp.sum(w_pre, -1)
    summed_rows = jnp.einsum(
        "wnso,onr->wnsr",
        w_pre.astype(jnp.bfloat16),
        prefix_value_rows,
        preferred_element_type=jnp.float32,
    )
    suffix_weight_rows = jnp.where(svalid, jnp.exp(suffix_score_rows - top_own[..., None]), 0.0)
    w_new = jnp.exp(fresh_score_rows - top_own)
    own_total = jnp.sum(suffix_weight_rows, -1) + w_new
    own_sum = jnp.einsum(
        "cjax,cxjq->cjaq",
        suffix_weight_rows.astype(jnp.bfloat16),
        suffix_value_rows,
        preferred_element_type=jnp.float32,
    )
    own_sum = (
        own_sum
        + w_new.astype(jnp.bfloat16).astype(jnp.float32)[..., None]
        * nvals.astype(jnp.float32)[:, :, None, :]
    )
    total = lax.dynamic_update_slice_in_dim(
        total,
        lax.dynamic_slice_in_dim(total, first_row, samples_per_part, 0) + own_total,
        first_row,
        0,
    )
    summed_rows = lax.dynamic_update_slice_in_dim(
        summed_rows,
        lax.dynamic_slice_in_dim(summed_rows, first_row, samples_per_part, 0) + own_sum,
        first_row,
        0,
    )
    top_flat = local_top.reshape(batch, HQ)
    total_flat = total.reshape(batch, HQ)
    summed_flat = summed_rows.reshape(batch, HQ, HEAD_SIZE)
    parts = (
        lax.all_to_all(top_flat[None], "mp", split_axis=2, concat_axis=0, tiled=True),
        lax.all_to_all(total_flat[None], "mp", split_axis=2, concat_axis=0, tiled=True),
        lax.all_to_all(summed_flat[None], "mp", split_axis=2, concat_axis=0, tiled=True),
    )
    best = jnp.max(parts[0], axis=0)
    factor = jnp.exp(parts[0] - best[None])
    whole_total = jnp.sum(factor * parts[1], axis=0)
    whole_summed = jnp.sum(factor[..., None] * parts[2], axis=0)
    items = parts[0].shape[1]
    attn = (
        (whole_summed / whole_total[..., None])
        .astype(jnp.bfloat16)
        .reshape(items, heads_dev * HEAD_SIZE)
    )
    proj = lax.psum_scatter(
        jnp.dot(attn, out_weight, preferred_element_type=jnp.float32),
        "mp",
        scatter_dimension=0,
        tiled=True,
    )
    stream = residual.astype(jnp.float32) + proj
    hidden = stream.astype(jnp.bfloat16)
    meansq = jnp.mean(stream * stream, axis=-1, keepdims=True)
    normed = (stream * lax.rsqrt(meansq + 1e-05) * norm_gain.astype(jnp.float32)[None, :]).astype(
        jnp.bfloat16
    )
    return (hidden, normed)


def solution(mesh):
    placed = (
        P(("dp", "mp"), None),
        P(("dp", "mp"), None),
        P(("dp", "mp"), None),
        P(("dp", "mp"), None),
        P(("dp", "mp"), None),
        P(("dp", "mp"), None, None),
        P(("dp", "mp"), None, None),
        P("dp"),
        P(("dp", "mp")),
        P(("dp", "mp"), None),
        P("mp", None),
        P(),
    )
    return jax.shard_map(
        local,
        mesh=mesh,
        in_specs=placed,
        out_specs=(P(("dp", "mp"), None), P(("dp", "mp"), None)),
        check_vma=False,
    )
```

profile of v0, /device:TPU:0, one launch (start us, length us, event | category | flops | bytes accessed | tf_op | source)
XLA Modules:
  0.0 110.2 jit_solution(15643182920238004057)
XLA Ops:
  7.2 0.0 copy-start
  7.2 0.0 copy-start.3
  7.2 0.0 copy-start.2
  7.2 0.0 copy-start.1
  7.9 1.0 copy.106
  8.9 15.1 %all-gather = bf16[4,1,4096]{2,1,0:T(2,128)(2,1)S(1)} all-gather(bf16[1,1,4096]{2,1,0:T(2,128)(2,1)} %bitcast.113), channel_id=1, replica_groups=mesh['dp'=8,'mp'=4] {'mp'}, dimensions={0}, use_global_device_ids=true | all-gather | bytes 40960 | tf_op jit(solution)/shard_map/all_gather | solution.py:35
  24.0 0.8 reduce.7
  24.8 0.2 reduce.6
  25.0 0.3 fusion.39
  25.4 0.1 copy.68
  26.2 0.9 copy.107
  27.1 0.2 fusion.40
  27.3 0.1 copy.70
  27.4 0.0 copy-done
  27.4 0.1 fusion.31
  27.6 0.1 copy.93
  27.7 0.1 copy.76
  27.8 0.2 fusion.12
  28.0 0.1 copy.105
  28.1 0.1 copy.78
  28.2 0.2 fusion.19
  28.3 0.1 copy.85
  28.4 0.1 copy.86
  28.6 0.7 copy.101
  29.3 4.7 %all-to-all-start.2 = ((f32[1,4,32]{1,0,2:T(1,128)}), f32[1,4,32]{1,0,2:T(1,128)S(1)}, u32[]{:S(2)}, u32[]{:S(2)}) async-start(f32[1,4,32]{1,0,2:T(1,128)} %bitcast.25), calls=%async_computation.2 | async-start | bytes 32768 | tf_op jit(solution)/shard_map/all_to_all | solution.py:118
  34.0 1.0 copy.108
  35.0 0.3 fusion.6
  35.3 0.7 copy.97
  36.0 0.1 copy.80
  36.1 0.9 copy.109
  37.0 0.7 convert_element_type.50
  37.7 1.9 %all-to-all-done.2 = f32[1,4,32]{1,0,2:T(1,128)S(1)} async-done(((f32[1,4,32]{1,0,2:T(1,128)}), f32[1,4,32]{1,0,2:T(1,128)S(1)}, u32[]{:S(2)}, u32[]{:S(2)}) %all-to-all-start.2) | async-done | bytes 544 | tf_op jit(solution)/shard_map/all_to_all | solution.py:118
  39.7 3.3 %all-to-all-start = ((f32[1,4,32]{1,0,2:T(1,128)}), f32[1,4,32]{1,0,2:T(1,128)S(1)}, u32[]{:S(2)}, u32[]{:S(2)}) async-start(f32[1,4,32]{1,0,2:T(1,128)} %bitcast.9), calls=%async_computation | async-start | bytes 32768 | tf_op jit(solution)/shard_map/all_to_all | solution.py:117
  42.9 0.2 fusion.4
  43.2 0.7 copy.82
  43.8 0.1 copy.102
  43.9 4.6 %all-to-all-done = f32[1,4,32]{1,0,2:T(1,128)S(1)} async-done(((f32[1,4,32]{1,0,2:T(1,128)}), f32[1,4,32]{1,0,2:T(1,128)S(1)}, u32[]{:S(2)}, u32[]{:S(2)}) %all-to-all-start) | async-done | bytes 544 | tf_op jit(solution)/shard_map/all_to_all | solution.py:117
  48.5 3.3 %all-to-all-start.1 = ((f32[1,4,32,128]{3,1,0,2:T(4,128)}), f32[1,4,32,128]{3,1,0,2:T(4,128)S(1)}, u32[]{:S(2)}, u32[]{:S(2)}) async-start(f32[1,4,32,128]{3,1,0,2:T(4,128)} %copy.82), calls=%async_computation.1 | async-start | bytes 131072 | tf_op jit(solution)/shard_map/all_to_all | solution.py:119
  51.8 0.0 all-reduce.3.cloned.1.call-start
  51.8 0.1 copy.98
  52.0 5.5 %all-to-all-done.1 = f32[1,4,32,128]{3,1,0,2:T(4,128)S(1)} async-done(((f32[1,4,32,128]{3,1,0,2:T(4,128)}), f32[1,4,32,128]{3,1,0,2:T(4,128)S(1)}, u32[]{:S(2)}, u32[]{:S(2)}) %all-to-all-start.1) | async-done | bytes 65568 | tf_op jit(solution)/shard_map/all_to_all | solution.py:119
  57.5 0.1 fusion.11
  57.6 0.1 fusion.29
  57.7 8.7 %fusion.22 = f32[4,8192]{1,0:T(4,128)} fusion(bf16[1024,8192]{1,0:T(8,128)(2,1)} %param.22, bf16[1,4,8,128]{3,2,1,0:T(8,128)(2,1)S(1)} %fusion.29), kind=kOutput, calls=%fused_computation.30 | convolution fusion | flops 67108864 | bytes 16916480 | tf_op jit(solution)/shard_map/dot_general | solution.py:132
  66.4 0.0 all-reduce.3.cloned.1.call-update
  66.4 0.0 copy-done.2
  66.4 0.0 copy-done.3
  66.4 0.6 dynamic-slice.4
  67.0 32.7 %all-reduce.3.cloned.1.call-done = f32[4,8192]{1,0:T(4,128)} async-done(((f32[4,8192]{1,0:T(4,128)}), f32[4,8192]{1,0:T(4,128)}) %all-reduce.3.cloned.1.call-update) | async-done | bytes 131088
  99.8 0.0 copy-done.1
  99.8 2.2 %multiply_reduce_fusion = (f32[]{:T(128)}, f32[1,8192]{1,0:T(1,128)S(1)}) fusion(f32[4,8192]{1,0:T(4,128)} %all-reduce.3.cloned.1.call-done, u32[]{:T(128)} %bitcast.33, bf16[1,8192]{1,0:T(2,128)(2,1)S(1)} %copy-done.1), kind=kLoop, calls=%fused_computation.22 | loop fusion | flops 32767 | bytes 81928 | tf_op jit(solution)/shard_map/reduce_sum | solution.py:139
  102.7 0.7 multiply_convert_fusion
  (15 shorter events, 0.2 us)
Async XLA Ops:
  7.2 20.2 %copy-start = (bf16[1,1024]{1,0:T(2,128)(2,1)S(1)}, bf16[1,1024]{1,0:T(2,128)(2,1)}, u32[]{:S(2)}) copy-start(bf16[1,1024]{1,0:T(2,128)(2,1)} %param.13) | copy-start | bytes 6148
  7.2 59.2 %copy-start.3 = (u32[32]{0:T(128)S(1)}, u32[32]{0:T(128)}, u32[]{:S(2)}) copy-start(u32[32]{0:T(128)} %constant.37) | copy-start | bytes 388
  7.2 59.2 %copy-start.2 = (bf16[8192]{0:T(1024)(128)(2,1)S(1)}, bf16[8192]{0:T(1024)(128)(2,1)}, u32[]{:S(2)}) copy-start(bf16[8192]{0:T(1024)(128)(2,1)} %param.23) | copy-start | bytes 49156
  7.2 92.6 %copy-start.1 = (bf16[1,8192]{1,0:T(2,128)(2,1)S(1)}, bf16[1,8192]{1,0:T(2,128)(2,1)}, u32[]{:S(2)}) copy-start(bf16[1,8192]{1,0:T(2,128)(2,1)} %param.21) | copy-start | bytes 49156
  29.3 10.3 %all-to-all-start.2 = ((f32[1,4,32]{1,0,2:T(1,128)}), f32[1,4,32]{1,0,2:T(1,128)S(1)}, u32[]{:S(2)}, u32[]{:S(2)}) async-start(f32[1,4,32]{1,0,2:T(1,128)} %bitcast.25), calls=%async_computation.2 | async-start | bytes 32768 | tf_op jit(solution)/shard_map/all_to_all | solution.py:118
  39.7 8.8 %all-to-all-start = ((f32[1,4,32]{1,0,2:T(1,128)}), f32[1,4,32]{1,0,2:T(1,128)S(1)}, u32[]{:S(2)}, u32[]{:S(2)}) async-start(f32[1,4,32]{1,0,2:T(1,128)} %bitcast.9), calls=%async_computation | async-start | bytes 32768 | tf_op jit(solution)/shard_map/all_to_all | solution.py:117
  48.5 9.0 %all-to-all-start.1 = ((f32[1,4,32,128]{3,1,0,2:T(4,128)}), f32[1,4,32,128]{3,1,0,2:T(4,128)S(1)}, u32[]{:S(2)}, u32[]{:S(2)}) async-start(f32[1,4,32,128]{3,1,0,2:T(4,128)} %copy.82), calls=%async_computation.1 | async-start | bytes 131072 | tf_op jit(solution)/shard_map/all_to_all | solution.py:119
  51.8 48.0 %all-reduce.3.cloned.1.call-start = ((), (), s32[]{:S(2)}) async-start(), calls=%async_computation.3 | async-start | bytes 262144
Sparse Core Ops, SparseCore 0:
  66.5 33.1 all-reduce.2
where the time goes:
time: 111 us; the launch traced here: 110 us
  waiting for transfers between devices  44.8 us (40%)
  between operations  16.2 us (15%)
  blocking collectives  15.1 us (14%)
  starting transfers between devices  11.3 us (10%)
  matrix products  9.91 us (9%)
  local copies, waits for them, and re-layouts  7.66 us (7%)
  other arithmetic  5.2 us (5%)
    unnamed x2, waiting for transfers between devices  32.7 us
    all_gather x1, blocking collectives, local(): queries = lax.all_gather(query_new, 'mp', axis=0, tiled=True)  15.1 us
    dot_general x1, matrix products, local(): jnp.dot(attn, out_weight, preferred_element_type=jnp.float32)  8.71 us
    all_to_all x1, waiting for transfers between devices, local(): lax.all_to_all(summed_flat[None], 'mp', split_axis=2, concat_axis=0, tile...  5.51 us
    all_to_all x1, starting transfers between devices, local(): lax.all_to_all(total_flat[None], 'mp', split_axis=2, concat_axis=0, tiled...  4.74 us
    all_to_all x1, waiting for transfers between devices, local(): lax.all_to_all(top_flat[None], 'mp', split_axis=2, concat_axis=0, tiled=T...  4.56 us
    unnamed x15, local copies, waits for them, and re-layouts  4.53 us
    all_to_all x1, starting transfers between devices, local(): lax.all_to_all(summed_flat[None], 'mp', split_axis=2, concat_axis=0, tile...  3.28 us
  transfers between devices with their start and end apart: 4, of which 4 were waited for; matrix products, arithmetic and copies ran while one was open for 5% of the time, Pallas kernels for 0%

commit v1 on v0

--- a/solution.py
+++ b/solution.py
@@ -114,7 +114,12 @@
     total_flat = total.reshape(batch, HQ)
     summed_flat = summed_rows.reshape(batch, HQ, HEAD_SIZE)
     parts = (
-        lax.all_to_all(top_flat[None], "mp", split_axis=2, concat_axis=0, tiled=True),
+        jnp.concatenate(
+            lax.all_to_all(
+                jnp.stack(jnp.split(top_flat[None], lax.axis_size("mp"), axis=2)), "mp", 0, 0
+            ),
+            axis=0,
+        ),
         lax.all_to_all(total_flat[None], "mp", split_axis=2, concat_axis=0, tiled=True),
         lax.all_to_all(summed_flat[None], "mp", split_axis=2, concat_axis=0, tiled=True),
     )

time: 111 us -> 111 us (level)
  no operation moved by 1% of the time
where the time goes in v1:
time: 111 us; the launch traced here: 110 us
  waiting for transfers between devices  44.7 us (40%)
  between operations  16.2 us (15%)
  blocking collectives  15.1 us (14%)
  starting transfers between devices  11.4 us (10%)
  matrix products  9.9 us (9%)
  local copies, waits for them, and re-layouts  7.11 us (6%)
  other arithmetic  5.8 us (5%)
    unnamed x2, waiting for transfers between devices  32.7 us
    all_gather x1, blocking collectives, local(): queries = lax.all_gather(query_new, 'mp', axis=0, tiled=True)  15.1 us
    dot_general x1, matrix products, local(): jnp.dot(attn, out_weight, preferred_element_type=jnp.float32)  8.71 us
    all_to_all x1, waiting for transfers between devices, local(): lax.all_to_all(summed_flat[None], 'mp', split_axis=2, concat_axis=0, tile...  5.61 us
    all_to_all x1, starting transfers between devices, local(): lax.all_to_all(total_flat[None], 'mp', split_axis=2, concat_axis=0, tiled...  4.74 us
    all_to_all x1, waiting for transfers between devices, local(): lax.all_to_all(jnp.stack(jnp.split(top_flat[None], lax.axis_size('mp'), a...  4.58 us
    unnamed x15, local copies, waits for them, and re-layouts  4.53 us
    all_to_all x1, starting transfers between devices, local(): lax.all_to_all(jnp.stack(jnp.split(top_flat[None], lax.axis_size('mp'), a...  3.32 us
  transfers between devices with their start and end apart: 4, of which 4 were waited for; matrix products, arithmetic and copies ran while one was open for 5% of the time, Pallas kernels for 0%

profile of v1, /device:TPU:0, one launch (start us, length us, event | category | flops | bytes accessed | tf_op | source)
XLA Modules:
  0.0 110.3 jit_solution(16687915880090200002)
XLA Ops:
  7.2 0.0 copy-start
  7.2 0.0 copy-start.3
  7.2 0.0 copy-start.2
  7.2 0.0 copy-start.1
  7.9 1.0 copy.95
  8.9 15.1 %all-gather = bf16[4,1,4096]{2,1,0:T(2,128)(2,1)S(1)} all-gather(bf16[1,1,4096]{2,1,0:T(2,128)(2,1)} %bitcast.116), channel_id=1, replica_groups=mesh['dp'=8,'mp'=4] {'mp'}, dimensions={0}, use_global_device_ids=true | all-gather | bytes 40960 | tf_op jit(solution)/shard_map/all_gather | solution.py:35
  24.0 0.8 reduce.7
  24.8 0.2 reduce.6
  25.0 0.3 fusion.39
  25.4 0.1 copy.63
  26.2 0.9 copy.96
  27.1 0.2 fusion.40
  27.3 0.1 copy.65
  27.4 0.0 copy-done
  27.4 0.1 fusion.31
  27.6 0.1 copy.85
  27.7 0.1 copy.68
  27.8 0.2 fusion.12
  28.0 0.1 copy.94
  28.1 0.1 copy.70
  28.2 0.2 fusion.19
  28.3 0.1 copy.77
  28.4 0.1 copy.78
  28.6 0.7 copy.91
  29.3 4.7 %all-to-all-start.2 = ((f32[1,4,32]{1,0,2:T(1,128)}), f32[1,4,32]{1,0,2:T(1,128)S(1)}, u32[]{:S(2)}, u32[]{:S(2)}) async-start(f32[1,4,32]{1,0,2:T(1,128)} %bitcast.26), calls=%async_computation.2 | async-start | bytes 32768 | tf_op jit(solution)/shard_map/all_to_all | solution.py:123
  34.0 0.1 copy.66
  34.1 0.1 broadcast_in_dim_reshape.9
  34.2 0.1 slice_bitcast_fusion.3
  34.3 1.0 copy.97
  35.3 0.3 fusion.6
  35.6 0.6 pad_maximum_fusion
  36.2 0.1 copy.72
  36.3 0.9 copy.98
  37.2 0.7 convert_element_type.50
  37.9 1.8 %all-to-all-done.2 = f32[1,4,32]{1,0,2:T(1,128)S(1)} async-done(((f32[1,4,32]{1,0,2:T(1,128)}), f32[1,4,32]{1,0,2:T(1,128)S(1)}, u32[]{:S(2)}, u32[]{:S(2)}) %all-to-all-start.2) | async-done | bytes 544 | tf_op jit(solution)/shard_map/all_to_all | solution.py:123
  39.7 3.3 %all-to-all-start = ((f32[4,1,4,8]{3,2,1,0:T(4,128)}), f32[4,1,4,8]{3,2,1,0:T(4,128)S(1)}, u32[]{:S(2)}, u32[]{:S(2)}) async-start(f32[4,1,4,8]{3,2,1,0:T(4,128)} %pad_maximum_fusion), calls=%async_computation | async-start | bytes 16384 | tf_op jit(solution)/shard_map/all_to_all | solution.py:118
  43.0 0.2 fusion.4
  43.2 0.7 copy.74
  43.9 0.1 copy.92
  44.0 4.6 %all-to-all-done = f32[4,1,4,8]{3,2,1,0:T(4,128)S(1)} async-done(((f32[4,1,4,8]{3,2,1,0:T(4,128)}), f32[4,1,4,8]{3,2,1,0:T(4,128)S(1)}, u32[]{:S(2)}, u32[]{:S(2)}) %all-to-all-start) | async-done | bytes 544 | tf_op jit(solution)/shard_map/all_to_all | solution.py:118
  48.6 3.3 %all-to-all-start.1 = ((f32[1,4,32,128]{3,1,0,2:T(4,128)}), f32[1,4,32,128]{3,1,0,2:T(4,128)S(1)}, u32[]{:S(2)}, u32[]{:S(2)}) async-start(f32[1,4,32,128]{3,1,0,2:T(4,128)} %copy.74), calls=%async_computation.1 | async-start | bytes 131072 | tf_op jit(solution)/shard_map/all_to_all | solution.py:124
  51.9 0.0 all-reduce.3.cloned.1.call-start
  52.0 5.6 %all-to-all-done.1 = f32[1,4,32,128]{3,1,0,2:T(4,128)S(1)} async-done(((f32[1,4,32,128]{3,1,0,2:T(4,128)}), f32[1,4,32,128]{3,1,0,2:T(4,128)S(1)}, u32[]{:S(2)}, u32[]{:S(2)}) %all-to-all-start.1) | async-done | bytes 65568 | tf_op jit(solution)/shard_map/all_to_all | solution.py:124
  57.6 0.1 fusion.11
  57.6 0.1 fusion.29
  57.7 8.7 %fusion.22 = f32[4,8192]{1,0:T(4,128)} fusion(bf16[1024,8192]{1,0:T(8,128)(2,1)} %param.22, bf16[1,4,8,128]{3,2,1,0:T(8,128)(2,1)S(1)} %fusion.29), kind=kOutput, calls=%fused_computation.30 | convolution fusion | flops 67108864 | bytes 16916480 | tf_op jit(solution)/shard_map/dot_general | solution.py:137
  66.4 0.0 all-reduce.3.cloned.1.call-update
  66.5 0.0 copy-done.2
  66.5 0.0 copy-done.3
  66.5 0.6 dynamic-slice.4
  67.1 32.7 %all-reduce.3.cloned.1.call-done = f32[4,8192]{1,0:T(4,128)} async-done(((f32[4,8192]{1,0:T(4,128)}), f32[4,8192]{1,0:T(4,128)}) %all-reduce.3.cloned.1.call-update) | async-done | bytes 131088
  99.8 0.0 copy-done.1
  99.8 2.2 %multiply_reduce_fusion = (f32[]{:T(128)}, f32[1,8192]{1,0:T(1,128)S(1)}) fusion(f32[4,8192]{1,0:T(4,128)} %all-reduce.3.cloned.1.call-done, u32[]{:T(128)} %bitcast.34, bf16[1,8192]{1,0:T(2,128)(2,1)S(1)} %copy-done.1), kind=kLoop, calls=%fused_computation.22 | loop fusion | flops 32767 | bytes 81928 | tf_op jit(solution)/shard_map/reduce_sum | solution.py:144
  102.7 0.7 multiply_convert_fusion
  (15 shorter events, 0.2 us)
Async XLA Ops:
  7.2 20.2 %copy-start = (bf16[1,1024]{1,0:T(2,128)(2,1)S(1)}, bf16[1,1024]{1,0:T(2,128)(2,1)}, u32[]{:S(2)}) copy-start(bf16[1,1024]{1,0:T(2,128)(2,1)} %param.13) | copy-start | bytes 6148
  7.2 59.3 %copy-start.3 = (u32[32]{0:T(128)S(1)}, u32[32]{0:T(128)}, u32[]{:S(2)}) copy-start(u32[32]{0:T(128)} %constant.37) | copy-start | bytes 388
  7.2 59.3 %copy-start.2 = (bf16[8192]{0:T(1024)(128)(2,1)S(1)}, bf16[8192]{0:T(1024)(128)(2,1)}, u32[]{:S(2)}) copy-start(bf16[8192]{0:T(1024)(128)(2,1)} %param.23) | copy-start | bytes 49156
  7.2 92.6 %copy-start.1 = (bf16[1,8192]{1,0:T(2,128)(2,1)S(1)}, bf16[1,8192]{1,0:T(2,128)(2,1)}, u32[]{:S(2)}) copy-start(bf16[1,8192]{1,0:T(2,128)(2,1)} %param.21) | copy-start | bytes 49156
  29.3 10.3 %all-to-all-start.2 = ((f32[1,4,32]{1,0,2:T(1,128)}), f32[1,4,32]{1,0,2:T(1,128)S(1)}, u32[]{:S(2)}, u32[]{:S(2)}) async-start(f32[1,4,32]{1,0,2:T(1,128)} %bitcast.26), calls=%async_computation.2 | async-start | bytes 32768 | tf_op jit(solution)/shard_map/all_to_all | solution.py:123
  39.7 8.9 %all-to-all-start = ((f32[4,1,4,8]{3,2,1,0:T(4,128)}), f32[4,1,4,8]{3,2,1,0:T(4,128)S(1)}, u32[]{:S(2)}, u32[]{:S(2)}) async-start(f32[4,1,4,8]{3,2,1,0:T(4,128)} %pad_maximum_fusion), calls=%async_computation | async-start | bytes 16384 | tf_op jit(solution)/shard_map/all_to_all | solution.py:118
  48.6 9.0 %all-to-all-start.1 = ((f32[1,4,32,128]{3,1,0,2:T(4,128)}), f32[1,4,32,128]{3,1,0,2:T(4,128)S(1)}, u32[]{:S(2)}, u32[]{:S(2)}) async-start(f32[1,4,32,128]{3,1,0,2:T(4,128)} %copy.74), calls=%async_computation.1 | async-start | bytes 131072 | tf_op jit(solution)/shard_map/all_to_all | solution.py:124
  51.9 48.0 %all-reduce.3.cloned.1.call-start = ((), (), s32[]{:S(2)}) async-start(), calls=%async_computation.3 | async-start | bytes 262144
Sparse Core Ops, SparseCore 0:
  66.6 33.1 all-reduce.2
